TPU v7x, 32 devices: a 4x2x2 block of a 4x4x8 slice. The times are simulated.
32 devices in a mesh: data: 4 (over y, z), fsdp: 8 (over x, core).
Axes of the slice: x: 4, y: 2, z: 2, core: 2. Of those that a mesh axis runs over, the one named last changes fastest.
The devices are a block of a 4x4x8 slice.
Arguments:
- hidden: bfloat16 [16384, 768], P('data'), parts along dimension 0
- targets: int32 [16384], P('data'), parts along dimension 0
- w_out: bfloat16 [50304, 768], P('fsdp')
Outputs:
- output 1: float32 [4], P('data'), parts along dimension 0
- output 2: float32 [16384, 768], P(('data', 'fsdp')), parts along dimension 0
- output 3: float32 [201216, 768], P(('data', 'fsdp')), parts along dimension 0
There are 4 independent parts. A program takes and returns all parts, laid end to end along the dimension named above; an argument that names none is the same for every part.
All inputs are finite; a program needn't handle non-finite values.
Results may differ from a plain program's by a relative error of at most 0.001.
Values are sent between devices in bfloat16 or wider.
A program may use at most 768 MiB of HBM per device.

v0:
```python
import jax
import jax.numpy as jnp
from jax import lax
from jax.sharding import PartitionSpec as P


def solution(mesh):
    def local_step(hidden, targets, w_blk):
        tok_group = hidden.shape[0]
        vocab_blk = w_blk.shape[0]
        vocab_start = lax.axis_index("fsdp") * vocab_blk
        logits = jnp.einsum("td,vd->tv", hidden, w_blk, preferred_element_type=jnp.float32)
        row_max = lax.pmax(jnp.max(logits, axis=1, keepdims=True), "fsdp")
        tgt_hit = (lax.broadcasted_iota(jnp.int32, (1, vocab_blk), 1) + vocab_start) == targets[:, None]
        exp_sum = jnp.sum(jnp.exp(logits - row_max), axis=1, keepdims=True)
        tgt_part = jnp.sum(jnp.where(tgt_hit, logits, 0.0), axis=1, keepdims=True)
        group_stats = lax.psum(jnp.concatenate([exp_sum, tgt_part], axis=1), "fsdp")
        log_norm = row_max + jnp.log(group_stats[:, :1])
        loss_val = (jnp.sum(log_norm - group_stats[:, 1:]) / tok_group).reshape(1)
        grad_logits = ((jnp.exp(logits - log_norm) - tgt_hit.astype(jnp.float32)) / tok_group).astype(jnp.bfloat16)
        grad_part = jnp.einsum("tv,vd->td", grad_logits, w_blk, preferred_element_type=jnp.float32)
        grad_hid = lax.psum_scatter(grad_part, "fsdp", scatter_dimension=0, tiled=True)
        grad_w = jnp.einsum("tv,td->vd", grad_logits, hidden, preferred_element_type=jnp.float32)
        return loss_val, grad_hid, grad_w

    return jax.shard_map(
        local_step,
        mesh=mesh,
        in_specs=(P("data", None), P("data"), P("fsdp", None)),
        out_specs=(P("data"), P(("data", "fsdp"), None), P(("data", "fsdp"), None)),
        check_vma=False,
    )
```

profile of v0, /device:TPU:81, one launch (start us, length us, event | category | flops | bytes accessed | tf_op | source)
XLA Modules:
  0.0 320.6 jit_solution(2346533819814612916)
XLA Ops:
  7.2 0.1 reduce-scatter.2.cloned.1.call-start
  7.3 0.0 copy-start
  7.3 51.6 %fusion.7 = (f32[4096]{0:T(1024)S(1)}, f32[4096,6288]{0,1:T(8,128)}) fusion(bf16[4096,768]{1,0:T(8,128)(2,1)} %param.3, bf16[6288,768]{1,0:T(8,128)(2,1)} %param.5), kind=kOutput, calls=%fused_computation.13 | convolution fusion | flops 39586426880 | bytes 118988800 | tf_op jit(solution)/shard_map/td,vd->tv/dot_general | solution.py:12
  58.9 24.0 %pmax.7 = f32[4096,1]{0,1:T(1,128)S(1)} all-reduce(f32[4096,1]{0,1:T(1,128)S(1)} %bitcast.16), channel_id=1, replica_groups=mesh['data'=4,'fsdp'=8] {'fsdp'}, use_global_device_ids=true, to_apply=%region_1.0 | all-reduce | flops 4096 | bytes 32768 | tf_op jit(solution)/shard_map/pmax | solution.py:13
  82.9 0.0 copy-done
  82.9 33.2 %exponential_reduce_fusion = (f32[4096]{0:T(1024)S(1)}, f32[4096]{0:T(1024)S(1)}) fusion(f32[4096,6288]{0,1:T(8,128)} %get-tuple-element.8, f32[4096]{0:T(1024)S(1)} %bitcast.12, s32[4096]{0:T(1024)S(1)} %copy-done, s32[6288]{0:T(1024)S(1)} %iota_add_fusion), kind=kLoop, calls=%fused_computation.6 | loop fusion | flops 128770048 | bytes 103113280 | tf_op jit(solution)/shard_map/reduce_sum | solution.py:15
  116.1 23.9 %psum.7 = f32[4096,2]{0,1:T(2,128)S(1)} all-reduce(f32[4096,2]{0,1:T(2,128)S(1)} %pad_maximum_fusion), channel_id=1, replica_groups=mesh['data'=4,'fsdp'=8] {'fsdp'}, use_global_device_ids=true, to_apply=%region_4.5 | all-reduce | flops 8192 | bytes 65536 | tf_op jit(solution)/shard_map/psum | solution.py:17
  140.0 0.6 fusion.5
  140.6 50.1 %fusion.3 = bf16[4096,6288]{0,1:T(8,128)(2,1)} fusion(f32[4096,6288]{0,1:T(8,128)} %get-tuple-element.8, f32[4096]{0:T(1024)S(1)} %bitcast.13, s32[4096]{0:T(1024)S(1)} %copy-done, s32[6288]{0:T(1024)S(1)} %iota_add_fusion), kind=kLoop, calls=%fused_computation.5 | loop fusion | flops 154533888 | bytes 154591808 | tf_op jit(solution)/shard_map/convert_element_type | solution.py:20
  190.7 49.2 %fusion.8 = f32[4096,768]{1,0:T(8,128)} fusion(bf16[4096,6288]{0,1:T(8,128)(2,1)} %fusion.3, bf16[6288,768]{1,0:T(8,128)(2,1)} %param.5), kind=kOutput, calls=%fused_computation.14 | convolution fusion | flops 39560675328 | bytes 73752576 | tf_op jit(solution)/shard_map/tv,vd->td/dot_general | solution.py:21
  240.0 0.1 reduce-scatter.2.cloned.1.call-update
  240.7 48.5 %fusion.9 = f32[6288,768]{1,0:T(8,128)} fusion(bf16[4096,6288]{0,1:T(8,128)(2,1)} %fusion.3, bf16[4096,768]{1,0:T(8,128)(2,1)} %param.3), kind=kOutput, calls=%fused_computation.15 | convolution fusion | flops 39560675328 | bytes 77119488 | tf_op jit(solution)/shard_map/tv,td->vd/dot_general | solution.py:23
  289.2 23.4 %reduce-scatter.2.cloned.1.call-done = f32[512,768]{1,0:T(8,128)} async-done(((f32[4096,768]{1,0:T(8,128)}), f32[512,768]{1,0:T(8,128)}) %reduce-scatter.2.cloned.1.call-update) | async-done | bytes 1572880 | tf_op jit(solution)/shard_map/reduce_scatter | solution.py:22
  (2 shorter events, 0.0 us)
Async XLA Ops:
  7.2 305.5 %reduce-scatter.2.cloned.1.call-start = ((), (), s32[]{:S(2)}) async-start(), calls=%async_computation.1 | async-start | bytes 14155776 | tf_op jit(solution)/shard_map/reduce_scatter | solution.py:22
  7.3 75.6 %copy-start = (s32[4096]{0:T(1024)S(1)}, s32[4096]{0:T(1024)}, u32[]{:S(2)}) copy-start(s32[4096]{0:T(1024)} %param.4) | copy-start | bytes 49156
Sparse Core Ops, SparseCore 0:
  240.2 72.4 reduce-scatter.1
where the time goes:
time: 321 us
  matrix products  149 us (46%)
  other arithmetic  84 us (26%)
  blocking collectives  47.8 us (15%)
  waiting for transfers between devices  23.5 us (7%)
  between operations  15.9 us (5%)
    dot_general x1, matrix products, local_step(): jnp.einsum('td,vd->tv', hidden, w_blk, preferred_element_type=jnp.float32)  51.6 us
    convert_element_type x1, other arithmetic, local_step(): ((jnp.exp(logits - log_norm) - tgt_hit.astype(jnp.float32)) / tok_group)....  50.1 us
    dot_general x1, matrix products, local_step(): jnp.einsum('tv,vd->td', grad_logits, w_blk, preferred_element_type=jnp.fl...  49.2 us
    dot_general x1, matrix products, local_step(): jnp.einsum('tv,td->vd', grad_logits, hidden, preferred_element_type=jnp.f...  48.5 us
    reduce_sum x1, other arithmetic, local_step(): exp_sum = jnp.sum(jnp.exp(logits - row_max), axis=1, keepdims=True)  33.2 us
    pmax x1, blocking collectives, local_step(): row_max = lax.pmax(jnp.max(logits, axis=1, keepdims=True), 'fsdp')  24 us
    psum x1, blocking collectives, local_step(): group_stats = lax.psum(jnp.concatenate([exp_sum, tgt_part], axis=1), 'fsdp')  23.9 us
    reduce_scatter x1, waiting for transfers between devices, local_step(): lax.psum_scatter(grad_part, 'fsdp', scatter_dimension=0, tiled=True)  23.4 us
  transfers between devices with their start and end apart: 1, of which 1 were waited for; matrix products, arithmetic and copies ran while one was open for 15% of the time, Pallas kernels for 0%

commit v1 on v0

v1 whole, which is shorter than its diff:
```python
import functools

import jax
import jax.numpy as jnp
from jax import lax
from jax.experimental import pallas as pl
from jax.experimental.pallas import tpu as pltpu
from jax.sharding import PartitionSpec as P

MESH = pl.DeviceIdType.MESH
AXIS = "fsdp"
TILE = 1024
VMEM_LIMIT = 67043328


def tiles_of(vocab, tile):
    count = vocab // tile
    return [(j * tile, tile if j < count - 1 else vocab - j * tile) for j in range(count)]


def stats_kernel(n, tile, h_ref, w_ref, tgt_ref, z_hbm, lse_ref, loss_ref, zbuf, stat, recv, zsem, send_sem, recv_sem):
    c = pl.program_id(0)
    p = lax.rem(c, 2)
    me = lax.axis_index(AXIS)
    vocab, t = w_ref.shape[0], h_ref.shape[0]

    @pl.when(c == 0)
    def _():
        barrier = pltpu.get_barrier_semaphore()
        for r in range(1, n):
            pl.semaphore_signal(barrier, inc=1, device_id={AXIS: lax.rem(me + r, n)}, device_id_type=MESH)
        pl.semaphore_wait(barrier, n - 1)
        stat[...] = jnp.zeros_like(stat)

    def send(chunk):
        for r in range(1, n):
            pltpu.make_async_remote_copy(
                src_ref=stat.at[chunk],
                dst_ref=recv.at[chunk, r - 1],
                send_sem=send_sem,
                recv_sem=recv_sem,
                device_id={AXIS: lax.rem(me + r, n)},
                device_id_type=MESH,
            ).start()

    @pl.when(c >= 1)
    def _():
        send(c - 1)

    @pl.when(c >= 2)
    def _():
        pltpu.make_async_copy(zbuf.at[p], z_hbm.at[c - 2], zsem.at[p]).wait()

    tgt = tgt_ref[c] - me * vocab
    m = s = hit_sum = None
    for r0, rows in tiles_of(vocab, tile):
        z = lax.dot_general(
            w_ref[r0 : r0 + rows, :], h_ref[...], (((1,), (1,)), ((), ())), preferred_element_type=jnp.float32
        )
        zbuf[p, r0 : r0 + rows, :] = z
        pltpu.make_async_copy(zbuf.at[p, pl.ds(r0, rows)], z_hbm.at[c, pl.ds(r0, rows)], zsem.at[p]).start()
        tile_max = jnp.max(z, axis=0, keepdims=True)
        new_m = tile_max if m is None else jnp.maximum(m, tile_max)
        tile_sum = jnp.sum(jnp.exp(z - new_m), axis=0, keepdims=True)
        hit = lax.broadcasted_iota(jnp.int32, (rows, t), 0) == tgt - r0
        tile_hit = jnp.sum(jnp.where(hit, z, 0.0), axis=0, keepdims=True)
        if m is None:
            s, hit_sum = tile_sum, tile_hit
        else:
            s = s * jnp.exp(m - new_m) + tile_sum
            hit_sum = hit_sum + tile_hit
        m = new_m
    stat[c, 0:1, :] = m
    stat[c, 1:2, :] = s
    stat[c, 2:3, :] = hit_sum

    @pl.when(c == n - 1)
    def _():
        send(c)
        pltpu.make_async_copy(zbuf.at[1 - p], z_hbm.at[c - 1], zsem.at[1 - p]).wait()
        pltpu.make_async_copy(zbuf.at[p], z_hbm.at[c], zsem.at[p]).wait()
        pltpu.make_async_copy(recv, recv, send_sem).wait()
        pltpu.make_async_copy(recv, recv, recv_sem).wait()
        total = jnp.zeros((1, 1), jnp.float32)
        for k in range(n):
            big = stat[k, 0:1, :]
            for r in range(n - 1):
                big = jnp.maximum(big, recv[k, r, 0:1, :])
            own = stat[k, 1:2, :] * jnp.exp(stat[k, 0:1, :] - big)
            parts = [recv[k, r, 1:2, :] * jnp.exp(recv[k, r, 0:1, :] - big) for r in range(n - 1)]
            sums = stat_sum(n, me, own, parts)
            target = stat[k, 2:3, :]
            for r in range(n - 1):
                target = target + recv[k, r, 2:3, :]
            lse = big + jnp.log(sums)
            lse_ref[k] = lse
            total = total + jnp.sum(lse - target, axis=1, keepdims=True)
        loss_ref[...] = jnp.broadcast_to(total / (n * t), loss_ref.shape)


def stat_sum(n, me, own, parts):
    total = None
    for a in range(n):
        r = lax.rem(me - a + n, n)
        term = own
        for k in range(1, n):
            term = jnp.where(r == k, parts[k - 1], term)
        total = term if total is None else total + term
    return total


def run_stats(n, tile, hidden, targets, w_blk, collective_id):
    tok, d = hidden.shape
    vocab = w_blk.shape[0]
    t = tok // n
    return pl.pallas_call(
        functools.partial(stats_kernel, n, tile),
        grid=(n,),
        in_specs=[
            pl.BlockSpec((t, d), lambda c: (c, 0)),
            pl.BlockSpec((vocab, d), lambda c: (0, 0), pipeline_mode=pl.Buffered(1)),
            pl.BlockSpec((n, 1, t), lambda c: (0, 0, 0)),
        ],
        out_specs=[
            pl.BlockSpec(memory_space=pl.ANY),
            pl.BlockSpec((n, 1, t), lambda c: (0, 0, 0)),
            pl.BlockSpec((8, 128), lambda c: (0, 0)),
        ],
        out_shape=[
            jax.ShapeDtypeStruct((n, vocab, t), jnp.float32),
            jax.ShapeDtypeStruct((n, 1, t), jnp.float32),
            jax.ShapeDtypeStruct((8, 128), jnp.float32),
        ],
        scratch_shapes=[
            pltpu.VMEM((2, vocab, t), jnp.float32),
            pltpu.VMEM((n, 8, t), jnp.float32),
            pltpu.VMEM((n, n - 1, 8, t), jnp.float32),
            pltpu.SemaphoreType.DMA((2,)),
            pltpu.SemaphoreType.DMA,
            pltpu.SemaphoreType.DMA,
        ],
        compiler_params=pltpu.CompilerParams(
            dimension_semantics=("arbitrary",),
            collective_id=collective_id,
            has_side_effects=True,
            vmem_limit_bytes=VMEM_LIMIT,
        ),
        name="stats",
    )(hidden, w_blk, targets)


def grad_kernel(
    n, tile, wt_hbm, h_hbm, z_hbm, lse_ref, tgt_ref, dht_ref, dw_hbm,
    wt, hbuf, zin, dz0, dz1, dw, hacc, from_partner, from_ring,
    wsem, hsem, zsem, dwsem, p_send, p_recv, r_send, r_recv,
):
    me = lax.axis_index(AXIS)
    nx = n // 2
    x, core = lax.div(me, 2), lax.rem(me, 2)
    sgn = 1 - 2 * core
    d, t = dht_ref.shape
    vocab = dw.shape[0]
    tiles = tiles_of(vocab, tile)
    last = len(tiles) - 1
    dz = (dz0, dz1)
    partner = 2 * x + (1 - core)
    ahead = 2 * lax.rem(x + sgn + nx, nx) + core
    behind = 2 * lax.rem(x - sgn + nx, nx) + core

    def chunk_of(s):
        q, mine = lax.div(s, 2), lax.rem(s, 2)
        e = sgn * (2 * mine - 1)
        off = jnp.where(q == 0, 2, jnp.where(q == 1, e, jnp.where(q == 2, -e, 0)))
        owner_core = core * mine + (1 - core) * (1 - mine)
        return 2 * lax.rem(x + off + nx, nx) + owner_core

    def z_copy(chunk, j):
        r0, rows = tiles[j]
        return pltpu.make_async_copy(
            z_hbm.at[chunk, pl.ds(r0, rows)], zin.at[j % 3, pl.ds(0, rows)], zsem.at[j % 3]
        )

    def h_copy(chunk, slot):
        return pltpu.make_async_copy(h_hbm.at[pl.ds(chunk * t, t)], hbuf.at[slot], hsem.at[slot])

    def make_dz(chunk, j):
        r0, rows = tiles[j]
        z = zin[j % 3, 0:rows, :]
        hit = lax.broadcasted_iota(jnp.int32, (rows, t), 0) == tgt_ref[chunk] - (me * vocab + r0)
        g = (jnp.exp(z - lse_ref[chunk]) - jnp.where(hit, 1.0, 0.0)) * (1.0 / (n * t))
        dz[j % 2][0:rows, :] = g.astype(jnp.bfloat16)

    first = chunk_of(0)
    w_copy = pltpu.make_async_copy(wt_hbm, wt, wsem)
    h_copy(first, 0).start()
    for j in range(3):
        z_copy(first, j).start()
    w_copy.start()

    barrier = pltpu.get_barrier_semaphore()
    for peer in (partner, ahead, behind):
        pl.semaphore_signal(barrier, inc=1, device_id={AXIS: peer}, device_id_type=MESH)
    pl.semaphore_wait(barrier, 3)

    def partner_copy(q):
        return pltpu.make_async_remote_copy(
            src_ref=hacc.at[0], dst_ref=from_partner.at[q], send_sem=p_send.at[q], recv_sem=p_recv.at[q],
            device_id={AXIS: partner}, device_id_type=MESH,
        )

    def ring_copy(q, peer):
        return pltpu.make_async_remote_copy(
            src_ref=hacc.at[1 + lax.rem(q, 2)], dst_ref=from_ring.at[q], send_sem=r_send.at[q], recv_sem=r_recv.at[q],
            device_id={AXIS: peer}, device_id_type=MESH,
        )

    step = max(r for r in range(16, 129, 16) if vocab % r == 0)

    def zero(i, carry):
        dw[pl.ds(i * step, step), :] = jnp.zeros((step, d), jnp.float32)
        return carry

    lax.fori_loop(0, vocab // step, zero, 0)
    pad = dz1.shape[0] - tiles[last][1]
    if pad:
        dz1[tiles[last][1] :, :] = jnp.zeros((pad, t), jnp.bfloat16)
    z_copy(first, 0).wait()
    make_dz(first, 0)
    w_copy.wait()

    def stage(s, carry):
        chunk, following = chunk_of(s), chunk_of(jnp.minimum(s + 1, n - 1))
        q, mine = lax.div(s, 2), lax.rem(s, 2)
        slot = lax.rem(s, 2)
        acc = mine * (1 + lax.rem(q, 2))
        pq, pmine = lax.div(s - 1, 2), lax.rem(s + 1, 2)
        pacc = 1 + lax.rem(pq, 2)

        @pl.when(s < n - 1)
        def _():
            h_copy(following, 1 - slot).start()

        @pl.when(jnp.logical_and(mine == 0, q >= 1))
        def _():
            partner_copy(q - 1).wait_send()

        @pl.when(jnp.logical_and(mine == 1, q >= 2))
        def _():
            ring_copy(q - 2, ahead).wait_send()

        h_copy(chunk, slot).wait()
        for j, (r0, rows) in enumerate(tiles):
            nxt = j + 1
            if nxt <= last:
                z_copy(chunk, nxt).wait()
                make_dz(chunk, nxt)
            else:

                @pl.when(s < n - 1)
                def _():
                    z_copy(following, 0).wait()

                make_dz(following, 0)
            cols = rows if j < last else dz1.shape[0]
            part = jnp.dot(wt[:, r0 : r0 + cols], dz[j % 2][0:cols, :], preferred_element_type=jnp.float32)
            if j == 0:
                hacc[acc] = part
            else:
                hacc[acc] = hacc[acc] + part
            dw[r0 : r0 + rows, :] = dw[r0 : r0 + rows, :] + jnp.dot(
                dz[j % 2][0:rows, :], hbuf[slot], preferred_element_type=jnp.float32
            )

            if j + 3 <= last:
                z_copy(chunk, j + 3).start()
            else:

                @pl.when(s < n - 1)
                def _():
                    z_copy(following, j + 3 - last - 1).start()

            @pl.when(s == n - 1)
            def _():
                pltpu.make_async_copy(dw.at[pl.ds(r0, rows)], dw_hbm.at[pl.ds(r0, rows)], dwsem).start()

            if j == 0:

                @pl.when(jnp.logical_and(s >= 1, pmine == 1))
                def _():
                    partner_copy(pq).wait_recv()
                    hacc[pacc] = hacc[pacc] + from_partner[pq]

                    @pl.when(pq == 1)
                    def _():
                        ring_copy(0, ahead).wait_recv()
                        hacc[pacc] = hacc[pacc] + from_ring[0]

            if j == 1:

                @pl.when(jnp.logical_and(s >= 1, pmine == 0))
                def _():
                    partner_copy(pq).start()

                @pl.when(jnp.logical_and(s >= 1, jnp.logical_and(pmine == 1, pq < 2)))
                def _():
                    ring_copy(pq, ahead).start()

                @pl.when(jnp.logical_and(s >= 1, jnp.logical_and(pmine == 1, pq == 2)))
                def _():
                    ring_copy(2, behind).start()

        return carry

    lax.fori_loop(0, n, stage, 0)

    partner_copy(3).wait_recv()
    ring_copy(1, ahead).wait_recv()
    total = hacc[2] + from_partner[3] + from_ring[1]
    ring_copy(2, behind).wait_recv()
    dht_ref[...] = total + from_ring[2]
    partner_copy(3).wait_send()
    ring_copy(2, behind).wait_send()
    pltpu.make_async_copy(dw, dw_hbm, dwsem).wait()


def run_grads(n, tile, w_t, hidden, z, lse, targets, collective_id):
    tok, d = hidden.shape
    vocab = z.shape[1]
    t = tok // n
    rows = tiles_of(vocab, tile)[-1][1]
    last_cols = w_t.shape[1] - (vocab - rows)
    any_spec = pl.BlockSpec(memory_space=pl.ANY)
    vmem_spec = pl.BlockSpec(memory_space=pltpu.VMEM)
    return pl.pallas_call(
        functools.partial(grad_kernel, n, tile),
        in_specs=[any_spec, any_spec, any_spec, vmem_spec, vmem_spec],
        out_specs=[vmem_spec, any_spec],
        out_shape=[
            jax.ShapeDtypeStruct((d, t), jnp.float32),
            jax.ShapeDtypeStruct((vocab, d), jnp.float32),
        ],
        scratch_shapes=[
            pltpu.VMEM(w_t.shape, jnp.bfloat16),
            pltpu.VMEM((2, t, d), jnp.bfloat16),
            pltpu.VMEM((3, rows, t), jnp.float32),
            pltpu.VMEM((tile, t), jnp.bfloat16),
            pltpu.VMEM((last_cols, t), jnp.bfloat16),
            pltpu.VMEM((vocab, d), jnp.float32),
            pltpu.VMEM((3, d, t), jnp.float32),
            pltpu.VMEM((4, d, t), jnp.float32),
            pltpu.VMEM((3, d, t), jnp.float32),
            pltpu.SemaphoreType.DMA,
            pltpu.SemaphoreType.DMA((2,)),
            pltpu.SemaphoreType.DMA((3,)),
            pltpu.SemaphoreType.DMA,
            pltpu.SemaphoreType.DMA((4,)),
            pltpu.SemaphoreType.DMA((4,)),
            pltpu.SemaphoreType.DMA((3,)),
            pltpu.SemaphoreType.DMA((3,)),
        ],
        compiler_params=pltpu.CompilerParams(
            collective_id=collective_id, has_side_effects=True, vmem_limit_bytes=VMEM_LIMIT
        ),
        name="grads",
    )(w_t, hidden, z, lse, targets)


def solution(mesh, tile=TILE):
    n = mesh.shape[AXIS]

    def local_step(hidden, targets, w_blk):
        tok = hidden.shape[0]
        vocab = w_blk.shape[0]
        tgt = targets.reshape(n, 1, tok // n)
        z, lse, loss = run_stats(n, tile, hidden, tgt, w_blk, 0)
        last_start = tiles_of(vocab, tile)[-1][0]
        padded = last_start + -(-(vocab - last_start) // 256) * 256
        w_t = jnp.pad(w_blk.T, ((0, 0), (0, padded - vocab)))
        dht, dw = run_grads(n, tile, w_t, hidden, z, lse, tgt, 1)
        return loss[0, :1], dht.T, dw

    return jax.shard_map(
        local_step,
        mesh=mesh,
        in_specs=(P("data", None), P("data"), P(AXIS, None)),
        out_specs=(P("data"), P(("data", AXIS), None), P(("data", AXIS), None)),
        check_vma=False,
    )
```

time: 321 us -> 273 us (0.85)
  Pallas kernels: 0 us -> 231 us
  matrix products: 149 us -> 0 us
  other arithmetic: 84 us -> 0 us
  blocking collectives: 47.8 us -> 0 us
  local copies, waits for them, and re-layouts: 0.01 us -> 40.7 us
  waiting for transfers between devices: 23.5 us -> 0 us
  between operations: 15.9 us -> 0.65 us
    pallas_call x0 -> x2, Pallas kernels: none -> 231 us  [the longest x1 159 us: run_grads(): pl.pallas_call(functools.partial(grad_kernel, n, tile), in_specs=[any_spe...]
    dot_general x3 -> x0, matrix products: 149 us -> none  [the longest x1 51.6 us: local_step(): jnp.einsum('td,vd->tv', hidden, w_blk, preferred_element_type=jnp.float32)]
    convert_element_type x1 -> x0, other arithmetic: 50.1 us -> none  [local_step(): ((jnp.exp(logits - log_norm) - tgt_hit.astype(jnp.float32)) / tok_group)....]
    reduce_sum x2 -> x0, other arithmetic: 33.8 us -> none  [the longest x1 33.2 us: local_step(): exp_sum = jnp.sum(jnp.exp(logits - row_max), axis=1, keepdims=True)]
    unnamed x2 -> x3, local copies, waits for them, and re-layouts: 0.01 us -> 31.3 us
    pmax x1 -> x0, blocking collectives: 24 us -> none  [local_step(): row_max = lax.pmax(jnp.max(logits, axis=1, keepdims=True), 'fsdp')]
    psum x1 -> x0, blocking collectives: 23.9 us -> none  [local_step(): group_stats = lax.psum(jnp.concatenate([exp_sum, tgt_part], axis=1), 'fsdp')]
    reduce_scatter x1 -> x0, waiting for transfers between devices: 23.4 us -> none  [local_step(): lax.psum_scatter(grad_part, 'fsdp', scatter_dimension=0, tiled=True)]
  transfers between devices with their start and end apart: 1 -> 0, of which waited for: 1 -> 0; matrix products, arithmetic and copies ran while one was open for 15% -> 0% of each run, Pallas kernels for 0% -> 0%
where the time goes in v1:
time: 273 us
  Pallas kernels  231 us (85%)
  local copies, waits for them, and re-layouts  40.7 us (15%)
    pallas_call x1, Pallas kernels, run_grads(): pl.pallas_call(functools.partial(grad_kernel, n, tile), in_specs=[any_spe...  159 us
    pallas_call x1, Pallas kernels, run_stats(): pl.pallas_call(functools.partial(stats_kernel, n, tile), grid=(n,), in_sp...  72.2 us
    unnamed x3, local copies, waits for them, and re-layouts  31.3 us
    pad x1, local copies, waits for them, and re-layouts, local_step(): w_t = jnp.pad(w_blk.T, ((0, 0), (0, padded - vocab)))  8.18 us

profile of v1, /device:TPU:81, one launch (start us, length us, event | category | flops | bytes accessed | tf_op | source)
XLA Modules:
  0.0 272.7 jit_solution(13264766691965342157)
XLA Ops:
  0.6 13.5 %copy.6 = bf16[6288,768]{0,1:T(8,128)(2,1)} copy(bf16[6288,768]{1,0:T(8,128)(2,1)} %w_ref.1) | data formatting | bytes 19316736 | tf_op args[2]
  14.2 8.2 %pad.4.wt_hbm = bf16[768,6400]{1,0:T(8,128)(2,1)} pad(bf16[768,6288]{1,0:T(8,128)(2,1)} %bitcast.4, bf16[]{:T(256)} %constant.2.clone.1), padding=0_0x0_112 | pad | bytes 19488770 | tf_op jit(solution)/shard_map/jit(_pad)/pad | solution.py:378
  22.4 72.2 %stats.1 = (f32[8,6288,512]{2,1,0:T(8,128)}, f32[8,1,512]{2,1,0:T(1,128)}, f32[8,128]{1,0:T(8,128)}) custom-call(bf16[4096,768]{1,0:T(8,128)(2,1)} %h_hbm.1, bf16[6288,768]{1,0:T(8,128)(2,1)} %w_ref.1, s32[8,1,512]{2,1,0:T(1,128)} %bitcast.6), custom_call_target="tpu_custom_call" | custom-call | tf_op jit(solution)/shard_map/stats/pallas_call | solution.py:116
  94.6 1.2 slice.3
  95.8 159.2 %grads.1 = (f32[768,512]{1,0:T(8,128)}, f32[6288,768]{1,0:T(8,128)}) custom-call(bf16[768,6400]{1,0:T(8,128)(2,1)} %pad.4.wt_hbm, bf16[4096,768]{1,0:T(8,128)(2,1)} %h_hbm.1, f32[8,6288,512]{2,1,0:T(8,128)} %get-tuple-element.9.z_hbm, f32[8,1,512]{2,1,0:T(1,128)} %get-tuple-element.10.lse_ref, s32[8,1,512]{2,1,0:T(1,128)} %bitcast.7), custom_call_target="tpu_custom_call" | custom-call | tf_op jit(solution)/shard_map/grads/pallas_call | solution.py:334
  254.9 3.0 %copy.7 = f32[512,768]{1,0:T(8,128)} copy(f32[512,768]{0,1:T(8,128)} %bitcast.5) | data formatting | bytes 3145728
  258.0 14.8 %copy.9 = f32[6288,768]{1,0:T(8,128)} copy(f32[6288,768]{1,0:T(8,128)} %get-tuple-element.21) | data formatting | bytes 38633472

commit v2 on v1

--- a/solution.py
+++ b/solution.py
@@ -10,12 +10,14 @@
 MESH = pl.DeviceIdType.MESH
 AXIS = "fsdp"
 TILE = 1024
+PIECE = 256
+ROWS = 528
 VMEM_LIMIT = 67043328
 
 
-def tiles_of(vocab, tile):
-    count = vocab // tile
-    return [(j * tile, tile if j < count - 1 else vocab - j * tile) for j in range(count)]
+def blocks_of(start, count, size):
+    blocks = max(count // size, 1)
+    return [(start + i * size, size if i < blocks - 1 else count - i * size) for i in range(blocks)]
 
 
 def stats_kernel(n, tile, h_ref, w_ref, tgt_ref, z_hbm, lse_ref, loss_ref, zbuf, stat, recv, zsem, send_sem, recv_sem):
@@ -52,27 +54,24 @@
         pltpu.make_async_copy(zbuf.at[p], z_hbm.at[c - 2], zsem.at[p]).wait()
 
     tgt = tgt_ref[c] - me * vocab
-    m = s = hit_sum = None
-    for r0, rows in tiles_of(vocab, tile):
+    maxima, totals, hits = [], [], []
+    for r0, rows in blocks_of(0, vocab, PIECE):
         z = lax.dot_general(
             w_ref[r0 : r0 + rows, :], h_ref[...], (((1,), (1,)), ((), ())), preferred_element_type=jnp.float32
         )
         zbuf[p, r0 : r0 + rows, :] = z
+        big = jnp.max(z, axis=0, keepdims=True)
+        total = jnp.sum(jnp.exp(z - big), axis=0, keepdims=True)
+        hit = lax.broadcasted_iota(jnp.int32, (rows, t), 0) == tgt - r0
+        maxima.append(big)
+        totals.append(total)
+        hits.append(jnp.sum(jnp.where(hit, z, 0.0), axis=0, keepdims=True))
+    for r0, rows in blocks_of(0, vocab, tile):
         pltpu.make_async_copy(zbuf.at[p, pl.ds(r0, rows)], z_hbm.at[c, pl.ds(r0, rows)], zsem.at[p]).start()
-        tile_max = jnp.max(z, axis=0, keepdims=True)
-        new_m = tile_max if m is None else jnp.maximum(m, tile_max)
-        tile_sum = jnp.sum(jnp.exp(z - new_m), axis=0, keepdims=True)
-        hit = lax.broadcasted_iota(jnp.int32, (rows, t), 0) == tgt - r0
-        tile_hit = jnp.sum(jnp.where(hit, z, 0.0), axis=0, keepdims=True)
-        if m is None:
-            s, hit_sum = tile_sum, tile_hit
-        else:
-            s = s * jnp.exp(m - new_m) + tile_sum
-            hit_sum = hit_sum + tile_hit
-        m = new_m
+    m = functools.reduce(jnp.maximum, maxima)
     stat[c, 0:1, :] = m
-    stat[c, 1:2, :] = s
-    stat[c, 2:3, :] = hit_sum
+    stat[c, 1:2, :] = sum(s * jnp.exp(big - m) for s, big in zip(totals, maxima))
+    stat[c, 2:3, :] = sum(hits)
 
     @pl.when(c == n - 1)
     def _():
@@ -149,20 +148,19 @@
     )(hidden, w_blk, targets)
 
 
-def grad_kernel(
-    n, tile, wt_hbm, h_hbm, z_hbm, lse_ref, tgt_ref, dht_ref, dw_hbm,
-    wt, hbuf, zin, dz0, dz1, dw, hacc, from_partner, from_ring,
-    wsem, hsem, zsem, dwsem, p_send, p_recv, r_send, r_recv,
+def hidden_grad_kernel(
+    n, tile, w_hbm, z_hbm, lse_ref, tgt_ref, dht_ref, dz_hbm,
+    w, zin, dz, hacc, from_partner, from_ring,
+    wsem, zsem, dzsem, p_send, p_recv, r_send, r_recv,
 ):
     me = lax.axis_index(AXIS)
     nx = n // 2
     x, core = lax.div(me, 2), lax.rem(me, 2)
     sgn = 1 - 2 * core
     d, t = dht_ref.shape
-    vocab = dw.shape[0]
-    tiles = tiles_of(vocab, tile)
+    vocab = w.shape[0]
+    tiles = blocks_of(0, vocab, tile)
     last = len(tiles) - 1
-    dz = (dz0, dz1)
     partner = 2 * x + (1 - core)
     ahead = 2 * lax.rem(x + sgn + nx, nx) + core
     behind = 2 * lax.rem(x - sgn + nx, nx) + core
@@ -180,19 +178,28 @@
             z_hbm.at[chunk, pl.ds(r0, rows)], zin.at[j % 3, pl.ds(0, rows)], zsem.at[j % 3]
         )
 
-    def h_copy(chunk, slot):
-        return pltpu.make_async_copy(h_hbm.at[pl.ds(chunk * t, t)], hbuf.at[slot], hsem.at[slot])
-
-    def make_dz(chunk, j):
+    def dz_copy(chunk, j):
         r0, rows = tiles[j]
-        z = zin[j % 3, 0:rows, :]
-        hit = lax.broadcasted_iota(jnp.int32, (rows, t), 0) == tgt_ref[chunk] - (me * vocab + r0)
-        g = (jnp.exp(z - lse_ref[chunk]) - jnp.where(hit, 1.0, 0.0)) * (1.0 / (n * t))
-        dz[j % 2][0:rows, :] = g.astype(jnp.bfloat16)
+        return pltpu.make_async_copy(
+            dz.at[j % 3, pl.ds(0, rows)],
+            dz_hbm.at[pl.ds(r0, rows), pl.ds(pl.multiple_of(chunk * t, t), t)],
+            dzsem.at[j % 3],
+        )
+
+    def partner_copy(q):
+        return pltpu.make_async_remote_copy(
+            src_ref=hacc.at[0], dst_ref=from_partner.at[q], send_sem=p_send.at[q], recv_sem=p_recv.at[q],
+            device_id={AXIS: partner}, device_id_type=MESH,
+        )
+
+    def ring_copy(q, peer):
+        return pltpu.make_async_remote_copy(
+            src_ref=hacc.at[1 + lax.rem(q, 2)], dst_ref=from_ring.at[q], send_sem=r_send.at[q], recv_sem=r_recv.at[q],
+            device_id={AXIS: peer}, device_id_type=MESH,
+        )
 
     first = chunk_of(0)
-    w_copy = pltpu.make_async_copy(wt_hbm, wt, wsem)
-    h_copy(first, 0).start()
+    w_copy = pltpu.make_async_copy(w_hbm, w, wsem)
     for j in range(3):
         z_copy(first, j).start()
     w_copy.start()
@@ -201,44 +208,15 @@
     for peer in (partner, ahead, behind):
         pl.semaphore_signal(barrier, inc=1, device_id={AXIS: peer}, device_id_type=MESH)
     pl.semaphore_wait(barrier, 3)
-
-    def partner_copy(q):
-        return pltpu.make_async_remote_copy(
-            src_ref=hacc.at[0], dst_ref=from_partner.at[q], send_sem=p_send.at[q], recv_sem=p_recv.at[q],
-            device_id={AXIS: partner}, device_id_type=MESH,
-        )
-
-    def ring_copy(q, peer):
-        return pltpu.make_async_remote_copy(
-            src_ref=hacc.at[1 + lax.rem(q, 2)], dst_ref=from_ring.at[q], send_sem=r_send.at[q], recv_sem=r_recv.at[q],
-            device_id={AXIS: peer}, device_id_type=MESH,
-        )
-
-    step = max(r for r in range(16, 129, 16) if vocab % r == 0)
-
-    def zero(i, carry):
-        dw[pl.ds(i * step, step), :] = jnp.zeros((step, d), jnp.float32)
-        return carry
-
-    lax.fori_loop(0, vocab // step, zero, 0)
-    pad = dz1.shape[0] - tiles[last][1]
-    if pad:
-        dz1[tiles[last][1] :, :] = jnp.zeros((pad, t), jnp.bfloat16)
-    z_copy(first, 0).wait()
-    make_dz(first, 0)
     w_copy.wait()
 
     def stage(s, carry):
         chunk, following = chunk_of(s), chunk_of(jnp.minimum(s + 1, n - 1))
         q, mine = lax.div(s, 2), lax.rem(s, 2)
-        slot = lax.rem(s, 2)
         acc = mine * (1 + lax.rem(q, 2))
         pq, pmine = lax.div(s - 1, 2), lax.rem(s + 1, 2)
         pacc = 1 + lax.rem(pq, 2)
-
-        @pl.when(s < n - 1)
-        def _():
-            h_copy(following, 1 - slot).start()
+        lse, tgt = lse_ref[chunk], tgt_ref[chunk] - me * vocab
 
         @pl.when(jnp.logical_and(mine == 0, q >= 1))
         def _():
@@ -248,28 +226,35 @@
         def _():
             ring_copy(q - 2, ahead).wait_send()
 
-        h_copy(chunk, slot).wait()
         for j, (r0, rows) in enumerate(tiles):
-            nxt = j + 1
-            if nxt <= last:
-                z_copy(chunk, nxt).wait()
-                make_dz(chunk, nxt)
+            z_copy(chunk, j).wait()
+            if j < 3:
+
+                @pl.when(s >= 1)
+                def _():
+                    dz_copy(chunk, j + last - 2).wait()
+
             else:
-
-                @pl.when(s < n - 1)
-                def _():
-                    z_copy(following, 0).wait()
-
-                make_dz(following, 0)
-            cols = rows if j < last else dz1.shape[0]
-            part = jnp.dot(wt[:, r0 : r0 + cols], dz[j % 2][0:cols, :], preferred_element_type=jnp.float32)
+                dz_copy(chunk, j - 3).wait()
+            parts = []
+            for b0, size in blocks_of(0, rows, PIECE):
+                z = zin[j % 3, b0 : b0 + size, :]
+                hit = lax.broadcasted_iota(jnp.int32, (size, t), 0) == tgt - (r0 + b0)
+                g = (jnp.exp(z - lse) - jnp.where(hit, 1.0, 0.0)) * (1.0 / (n * t))
+                g = g.astype(jnp.bfloat16)
+                dz[j % 3, b0 : b0 + size, :] = g
+                parts.append(g)
+            part = lax.dot_general(
+                w[r0 : r0 + rows, :],
+                jnp.concatenate(parts, axis=0),
+                (((0,), (0,)), ((), ())),
+                preferred_element_type=jnp.float32,
+            )
             if j == 0:
                 hacc[acc] = part
             else:
                 hacc[acc] = hacc[acc] + part
-            dw[r0 : r0 + rows, :] = dw[r0 : r0 + rows, :] + jnp.dot(
-                dz[j % 2][0:rows, :], hbuf[slot], preferred_element_type=jnp.float32
-            )
+            dz_copy(chunk, j).start()
 
             if j + 3 <= last:
                 z_copy(chunk, j + 3).start()
@@ -277,11 +262,7 @@
 
                 @pl.when(s < n - 1)
                 def _():
-                    z_copy(following, j + 3 - last - 1).start()
-
-            @pl.when(s == n - 1)
-            def _():
-                pltpu.make_async_copy(dw.at[pl.ds(r0, rows)], dw_hbm.at[pl.ds(r0, rows)], dwsem).start()
+                    z_copy(following, j + 2 - last).start()
 
             if j == 0:
 
@@ -313,46 +294,42 @@
 
     lax.fori_loop(0, n, stage, 0)
 
+    for j in range(last - 2, last + 1):
+        dz_copy(chunk_of(n - 1), j).wait()
     partner_copy(3).wait_recv()
+    total = hacc[2] + from_partner[3]
     ring_copy(1, ahead).wait_recv()
-    total = hacc[2] + from_partner[3] + from_ring[1]
+    total = total + from_ring[1]
     ring_copy(2, behind).wait_recv()
     dht_ref[...] = total + from_ring[2]
     partner_copy(3).wait_send()
     ring_copy(2, behind).wait_send()
-    pltpu.make_async_copy(dw, dw_hbm, dwsem).wait()
-
-
-def run_grads(n, tile, w_t, hidden, z, lse, targets, collective_id):
-    tok, d = hidden.shape
-    vocab = z.shape[1]
-    t = tok // n
-    rows = tiles_of(vocab, tile)[-1][1]
-    last_cols = w_t.shape[1] - (vocab - rows)
+
+
+def run_hidden_grad(n, tile, w_blk, z, lse, targets, collective_id):
+    vocab, d = w_blk.shape
+    t = z.shape[2]
+    rows = blocks_of(0, vocab, tile)[-1][1]
     any_spec = pl.BlockSpec(memory_space=pl.ANY)
     vmem_spec = pl.BlockSpec(memory_space=pltpu.VMEM)
     return pl.pallas_call(
-        functools.partial(grad_kernel, n, tile),
-        in_specs=[any_spec, any_spec, any_spec, vmem_spec, vmem_spec],
+        functools.partial(hidden_grad_kernel, n, tile),
+        in_specs=[any_spec, any_spec, vmem_spec, vmem_spec],
         out_specs=[vmem_spec, any_spec],
         out_shape=[
             jax.ShapeDtypeStruct((d, t), jnp.float32),
-            jax.ShapeDtypeStruct((vocab, d), jnp.float32),
+            jax.ShapeDtypeStruct((vocab, n * t), jnp.bfloat16),
         ],
         scratch_shapes=[
-            pltpu.VMEM(w_t.shape, jnp.bfloat16),
-            pltpu.VMEM((2, t, d), jnp.bfloat16),
+            pltpu.VMEM((vocab, d), jnp.bfloat16),
             pltpu.VMEM((3, rows, t), jnp.float32),
-            pltpu.VMEM((tile, t), jnp.bfloat16),
-            pltpu.VMEM((last_cols, t), jnp.bfloat16),
-            pltpu.VMEM((vocab, d), jnp.float32),
+            pltpu.VMEM((3, rows, t), jnp.bfloat16),
             pltpu.VMEM((3, d, t), jnp.float32),
             pltpu.VMEM((4, d, t), jnp.float32),
             pltpu.VMEM((3, d, t), jnp.float32),
             pltpu.SemaphoreType.DMA,
-            pltpu.SemaphoreType.DMA((2,)),
             pltpu.SemaphoreType.DMA((3,)),
-            pltpu.SemaphoreType.DMA,
+            pltpu.SemaphoreType.DMA((3,)),
             pltpu.SemaphoreType.DMA((4,)),
             pltpu.SemaphoreType.DMA((4,)),
             pltpu.SemaphoreType.DMA((3,)),
@@ -361,23 +338,40 @@
         compiler_params=pltpu.CompilerParams(
             collective_id=collective_id, has_side_effects=True, vmem_limit_bytes=VMEM_LIMIT
         ),
-        name="grads",
-    )(w_t, hidden, z, lse, targets)
+        name="hidden_grad",
+    )(w_blk, z, lse, targets)
+
+
+def weight_grad_kernel(dz_ref, h_ref, dw_ref):
+    dw_ref[...] = jnp.dot(dz_ref[...], h_ref[...], preferred_element_type=jnp.float32)
+
+
+def run_weight_grad(dz, hidden):
+    vocab, tok = dz.shape
+    d = hidden.shape[1]
+    rows = min(ROWS, vocab)
+    return pl.pallas_call(
+        weight_grad_kernel,
+        grid=(pl.cdiv(vocab, rows),),
+        in_specs=[
+            pl.BlockSpec((rows, tok), lambda i: (i, 0)),
+            pl.BlockSpec((tok, d), lambda i: (0, 0), pipeline_mode=pl.Buffered(1)),
+        ],
+        out_specs=pl.BlockSpec((rows, d), lambda i: (i, 0)),
+        out_shape=jax.ShapeDtypeStruct((vocab, d), jnp.float32),
+        compiler_params=pltpu.CompilerParams(dimension_semantics=("arbitrary",), vmem_limit_bytes=VMEM_LIMIT),
+        name="weight_grad",
+    )(dz, hidden)
 
 
 def solution(mesh, tile=TILE):
     n = mesh.shape[AXIS]
 
     def local_step(hidden, targets, w_blk):
-        tok = hidden.shape[0]
-        vocab = w_blk.shape[0]
-        tgt = targets.reshape(n, 1, tok // n)
+        tgt = targets.reshape(n, 1, hidden.shape[0] // n)
         z, lse, loss = run_stats(n, tile, hidden, tgt, w_blk, 0)
-        last_start = tiles_of(vocab, tile)[-1][0]
-        padded = last_start + -(-(vocab - last_start) // 256) * 256
-        w_t = jnp.pad(w_blk.T, ((0, 0), (0, padded - vocab)))
-        dht, dw = run_grads(n, tile, w_t, hidden, z, lse, tgt, 1)
-        return loss[0, :1], dht.T, dw
+        dht, dz = run_hidden_grad(n, tile, w_blk, z, lse, tgt, 1)
+        return loss[0, :1], dht.T, run_weight_grad(dz, hidden)
 
     return jax.shard_map(
         local_step,

time: 273 us -> 195 us (0.71)
  Pallas kernels: 231 us -> 190 us
  local copies, waits for them, and re-layouts: 40.7 us -> 4.21 us
    pallas_call x1 -> x2, Pallas kernels: 159 us -> 128 us  [the longest x1 80.3 us: run_hidden_grad(): pl.pallas_call(functools.partial(hidden_grad_kernel, n, tile), in_specs=[...]
    unnamed x3 -> x1, local copies, waits for them, and re-layouts: 31.3 us -> 3.02 us
    pallas_call x1, Pallas kernels: 72.2 us -> 62.2 us  [run_stats(): pl.pallas_call(functools.partial(stats_kernel, n, tile), grid=(n,), in_sp...]
    pad x1 -> x0, local copies, waits for them, and re-layouts: 8.18 us -> none  [local_step(): w_t = jnp.pad(w_blk.T, ((0, 0), (0, padded - vocab)))]
where the time goes in v2:
time: 195 us
  Pallas kernels  190 us (97%)
  local copies, waits for them, and re-layouts  4.21 us (2%)
    pallas_call x1, Pallas kernels, run_hidden_grad(): pl.pallas_call(functools.partial(hidden_grad_kernel, n, tile), in_specs=[...  80.3 us
    pallas_call x1, Pallas kernels, run_stats(): pl.pallas_call(functools.partial(stats_kernel, n, tile), grid=(n,), in_sp...  62.2 us
    pallas_call x1, Pallas kernels, run_weight_grad(): pl.pallas_call(weight_grad_kernel, grid=(pl.cdiv(vocab, rows),), in_specs...  47.5 us

profile of v2, /device:TPU:81, one launch (start us, length us, event | category | flops | bytes accessed | tf_op | source)
XLA Modules:
  0.0 194.9 jit_solution(15673195696245147413)
XLA Ops:
  0.6 62.2 %stats.1 = (f32[8,6288,512]{2,1,0:T(8,128)}, f32[8,1,512]{2,1,0:T(1,128)}, f32[8,128]{1,0:T(8,128)}) custom-call(bf16[4096,768]{1,0:T(8,128)(2,1)} %h_ref.3, bf16[6288,768]{1,0:T(8,128)(2,1)} %w_hbm.1, s32[8,1,512]{2,1,0:T(1,128)} %bitcast.4), custom_call_target="tpu_custom_call" | custom-call | tf_op jit(solution)/shard_map/stats/pallas_call | solution.py:115
  62.9 1.2 slice.3
  64.1 80.3 %hidden_grad.1 = (f32[768,512]{1,0:T(8,128)}, bf16[6288,4096]{1,0:T(8,128)(2,1)}) custom-call(bf16[6288,768]{1,0:T(8,128)(2,1)} %w_hbm.1, f32[8,6288,512]{2,1,0:T(8,128)} %get-tuple-element.9.z_hbm, f32[8,1,512]{2,1,0:T(1,128)} %get-tuple-element.10.lse_ref, s32[8,1,512]{2,1,0:T(1,128)} %bitcast.5), custom_call_target="tpu_custom_call" | custom-call | tf_op jit(solution)/shard_map/hidden_grad/pallas_call | solution.py:315
  144.3 3.0 %copy.6 = f32[512,768]{1,0:T(8,128)} copy(f32[512,768]{0,1:T(8,128)} %bitcast.3) | data formatting | bytes 3145728
  147.3 47.5 %weight_grad.1 = f32[6288,768]{1,0:T(8,128)} custom-call(bf16[6288,4096]{1,0:T(8,128)(2,1)} %get-tuple-element.12.dz_ref, bf16[4096,768]{1,0:T(8,128)(2,1)} %h_ref.3), custom_call_target="tpu_custom_call" | custom-call | tf_op jit(solution)/shard_map/weight_grad/pallas_call | solution.py:353

commit v3 on v2

--- a/solution.py
+++ b/solution.py
@@ -20,19 +20,30 @@
     return [(start + i * size, size if i < blocks - 1 else count - i * size) for i in range(blocks)]
 
 
-def stats_kernel(n, tile, h_ref, w_ref, tgt_ref, z_hbm, lse_ref, loss_ref, zbuf, stat, recv, zsem, send_sem, recv_sem):
+def stats_kernel(
+    n, tile, h_ref, w_hbm, tgt_ref, z_hbm, lse_ref, loss_ref, w_ref, zbuf, stat, recv, wsem, zsem, send_sem, recv_sem
+):
     c = pl.program_id(0)
     p = lax.rem(c, 2)
     me = lax.axis_index(AXIS)
     vocab, t = w_ref.shape[0], h_ref.shape[0]
 
+    halves = blocks_of(0, vocab, -(-vocab // (2 * PIECE)) * PIECE)
+
+    def w_copy(i):
+        r0, rows = halves[i]
+        return pltpu.make_async_copy(w_hbm.at[pl.ds(r0, rows)], w_ref.at[pl.ds(r0, rows)], wsem.at[i])
+
     @pl.when(c == 0)
     def _():
+        for i in range(len(halves)):
+            w_copy(i).start()
         barrier = pltpu.get_barrier_semaphore()
         for r in range(1, n):
             pl.semaphore_signal(barrier, inc=1, device_id={AXIS: lax.rem(me + r, n)}, device_id_type=MESH)
         pl.semaphore_wait(barrier, n - 1)
         stat[...] = jnp.zeros_like(stat)
+        w_copy(0).wait()
 
     def send(chunk):
         for r in range(1, n):
@@ -56,6 +67,12 @@
     tgt = tgt_ref[c] - me * vocab
     maxima, totals, hits = [], [], []
     for r0, rows in blocks_of(0, vocab, PIECE):
+        if len(halves) > 1 and r0 == halves[1][0]:
+
+            @pl.when(c == 0)
+            def _():
+                w_copy(1).wait()
+
         z = lax.dot_general(
             w_ref[r0 : r0 + rows, :], h_ref[...], (((1,), (1,)), ((), ())), preferred_element_type=jnp.float32
         )
@@ -80,7 +97,7 @@
         pltpu.make_async_copy(zbuf.at[p], z_hbm.at[c], zsem.at[p]).wait()
         pltpu.make_async_copy(recv, recv, send_sem).wait()
         pltpu.make_async_copy(recv, recv, recv_sem).wait()
-        total = jnp.zeros((1, 1), jnp.float32)
+        total = jnp.float32(0.0)
         for k in range(n):
             big = stat[k, 0:1, :]
             for r in range(n - 1):
@@ -93,8 +110,8 @@
                 target = target + recv[k, r, 2:3, :]
             lse = big + jnp.log(sums)
             lse_ref[k] = lse
-            total = total + jnp.sum(lse - target, axis=1, keepdims=True)
-        loss_ref[...] = jnp.broadcast_to(total / (n * t), loss_ref.shape)
+            total = total + jnp.sum(lse - target)
+        loss_ref[0] = total * (1.0 / (n * t))
 
 
 def stat_sum(n, me, own, parts):
@@ -117,23 +134,25 @@
         grid=(n,),
         in_specs=[
             pl.BlockSpec((t, d), lambda c: (c, 0)),
-            pl.BlockSpec((vocab, d), lambda c: (0, 0), pipeline_mode=pl.Buffered(1)),
+            pl.BlockSpec(memory_space=pl.ANY),
             pl.BlockSpec((n, 1, t), lambda c: (0, 0, 0)),
         ],
         out_specs=[
             pl.BlockSpec(memory_space=pl.ANY),
             pl.BlockSpec((n, 1, t), lambda c: (0, 0, 0)),
-            pl.BlockSpec((8, 128), lambda c: (0, 0)),
+            pl.BlockSpec(memory_space=pltpu.SMEM),
         ],
         out_shape=[
             jax.ShapeDtypeStruct((n, vocab, t), jnp.float32),
             jax.ShapeDtypeStruct((n, 1, t), jnp.float32),
-            jax.ShapeDtypeStruct((8, 128), jnp.float32),
+            jax.ShapeDtypeStruct((1,), jnp.float32),
         ],
         scratch_shapes=[
+            pltpu.VMEM((vocab, d), jnp.bfloat16),
             pltpu.VMEM((2, vocab, t), jnp.float32),
             pltpu.VMEM((n, 8, t), jnp.float32),
             pltpu.VMEM((n, n - 1, 8, t), jnp.float32),
+            pltpu.SemaphoreType.DMA((2,)),
             pltpu.SemaphoreType.DMA((2,)),
             pltpu.SemaphoreType.DMA,
             pltpu.SemaphoreType.DMA,
@@ -149,9 +168,9 @@
 
 
 def hidden_grad_kernel(
-    n, tile, w_hbm, z_hbm, lse_ref, tgt_ref, dht_ref, dz_hbm,
-    w, zin, dz, hacc, from_partner, from_ring,
-    wsem, zsem, dzsem, p_send, p_recv, r_send, r_recv,
+    n, tile, rows_w, blocks_w, w_hbm, z_hbm, h_hbm, lse_ref, tgt_ref, dht_ref, dz_hbm, dw_hbm,
+    w, zin, dz, hacc, from_partner, from_ring, h, dzb, dwb,
+    wsem, zsem, dzsem, p_send, p_recv, r_send, r_recv, hsem, bsem, dwsem,
 ):
     me = lax.axis_index(AXIS)
     nx = n // 2
@@ -198,6 +217,17 @@
             device_id={AXIS: peer}, device_id_type=MESH,
         )
 
+    def block_copy(i):
+        return pltpu.make_async_copy(
+            dz_hbm.at[pl.ds(i * rows_w, rows_w)], dzb.at[lax.rem(i, 2)], bsem.at[lax.rem(i, 2)]
+        )
+
+    def dw_copy(i):
+        return pltpu.make_async_copy(
+            dwb.at[lax.rem(i, 2)], dw_hbm.at[pl.ds(i * rows_w, rows_w)], dwsem.at[lax.rem(i, 2)]
+        )
+
+    h_copy = pltpu.make_async_copy(h_hbm, h, hsem)
     first = chunk_of(0)
     w_copy = pltpu.make_async_copy(w_hbm, w, wsem)
     for j in range(3):
@@ -209,6 +239,7 @@
         pl.semaphore_signal(barrier, inc=1, device_id={AXIS: peer}, device_id_type=MESH)
     pl.semaphore_wait(barrier, 3)
     w_copy.wait()
+    h_copy.start()
 
     def stage(s, carry):
         chunk, following = chunk_of(s), chunk_of(jnp.minimum(s + 1, n - 1))
@@ -236,6 +267,12 @@
 
             else:
                 dz_copy(chunk, j - 3).wait()
+                if j == 3:
+
+                    @pl.when(s == n - 1)
+                    def _():
+                        block_copy(0).start()
+
             parts = []
             for b0, size in blocks_of(0, rows, PIECE):
                 z = zin[j % 3, b0 : b0 + size, :]
@@ -271,10 +308,10 @@
                     partner_copy(pq).wait_recv()
                     hacc[pacc] = hacc[pacc] + from_partner[pq]
 
-                    @pl.when(pq == 1)
-                    def _():
-                        ring_copy(0, ahead).wait_recv()
-                        hacc[pacc] = hacc[pacc] + from_ring[0]
+                @pl.when(s == 5)
+                def _():
+                    ring_copy(0, ahead).wait_recv()
+                    hacc[2] = hacc[2] + from_ring[0]
 
             if j == 1:
 
@@ -282,11 +319,15 @@
                 def _():
                     partner_copy(pq).start()
 
-                @pl.when(jnp.logical_and(s >= 1, jnp.logical_and(pmine == 1, pq < 2)))
-                def _():
-                    ring_copy(pq, ahead).start()
-
-                @pl.when(jnp.logical_and(s >= 1, jnp.logical_and(pmine == 1, pq == 2)))
+                @pl.when(s == 2)
+                def _():
+                    ring_copy(0, ahead).start()
+
+                @pl.when(s == 5)
+                def _():
+                    ring_copy(1, ahead).start()
+
+                @pl.when(s == 6)
                 def _():
                     ring_copy(2, behind).start()
 
@@ -296,6 +337,25 @@
 
     for j in range(last - 2, last + 1):
         dz_copy(chunk_of(n - 1), j).wait()
+    h_copy.wait()
+
+    def block(i, carry):
+        slot = lax.rem(i, 2)
+
+        @pl.when(i + 1 < blocks_w)
+        def _():
+            block_copy(i + 1).start()
+
+        @pl.when(i >= 2)
+        def _():
+            dw_copy(i - 2).wait()
+
+        block_copy(i).wait()
+        dwb[slot] = jnp.dot(dzb[slot], h[...], preferred_element_type=jnp.float32)
+        dw_copy(i).start()
+        return carry
+
+    lax.fori_loop(0, blocks_w, block, 0)
     partner_copy(3).wait_recv()
     total = hacc[2] + from_partner[3]
     ring_copy(1, ahead).wait_recv()
@@ -304,21 +364,24 @@
     dht_ref[...] = total + from_ring[2]
     partner_copy(3).wait_send()
     ring_copy(2, behind).wait_send()
-
-
-def run_hidden_grad(n, tile, w_blk, z, lse, targets, collective_id):
+    for i in range(max(blocks_w - 2, 0), blocks_w):
+        dw_copy(i).wait()
+
+
+def run_hidden_grad(n, tile, rows_w, blocks_w, w_blk, z, hidden, lse, targets, collective_id):
     vocab, d = w_blk.shape
     t = z.shape[2]
     rows = blocks_of(0, vocab, tile)[-1][1]
     any_spec = pl.BlockSpec(memory_space=pl.ANY)
     vmem_spec = pl.BlockSpec(memory_space=pltpu.VMEM)
     return pl.pallas_call(
-        functools.partial(hidden_grad_kernel, n, tile),
-        in_specs=[any_spec, any_spec, vmem_spec, vmem_spec],
-        out_specs=[vmem_spec, any_spec],
+        functools.partial(hidden_grad_kernel, n, tile, rows_w, blocks_w),
+        in_specs=[any_spec, any_spec, any_spec, vmem_spec, vmem_spec],
+        out_specs=[vmem_spec, any_spec, any_spec],
         out_shape=[
             jax.ShapeDtypeStruct((d, t), jnp.float32),
             jax.ShapeDtypeStruct((vocab, n * t), jnp.bfloat16),
+            jax.ShapeDtypeStruct((blocks_w * rows_w, d), jnp.float32),
         ],
         scratch_shapes=[
             pltpu.VMEM((vocab, d), jnp.bfloat16),
@@ -327,6 +390,9 @@
             pltpu.VMEM((3, d, t), jnp.float32),
             pltpu.VMEM((4, d, t), jnp.float32),
             pltpu.VMEM((3, d, t), jnp.float32),
+            pltpu.VMEM((n * t, d), jnp.bfloat16),
+            pltpu.VMEM((2, rows_w, n * t), jnp.bfloat16),
+            pltpu.VMEM((2, rows_w, d), jnp.float32),
             pltpu.SemaphoreType.DMA,
             pltpu.SemaphoreType.DMA((3,)),
             pltpu.SemaphoreType.DMA((3,)),
@@ -334,44 +400,110 @@
             pltpu.SemaphoreType.DMA((4,)),
             pltpu.SemaphoreType.DMA((3,)),
             pltpu.SemaphoreType.DMA((3,)),
+            pltpu.SemaphoreType.DMA,
+            pltpu.SemaphoreType.DMA((2,)),
+            pltpu.SemaphoreType.DMA((2,)),
         ],
         compiler_params=pltpu.CompilerParams(
             collective_id=collective_id, has_side_effects=True, vmem_limit_bytes=VMEM_LIMIT
         ),
         name="hidden_grad",
-    )(w_blk, z, lse, targets)
-
-
-def weight_grad_kernel(dz_ref, h_ref, dw_ref):
-    dw_ref[...] = jnp.dot(dz_ref[...], h_ref[...], preferred_element_type=jnp.float32)
-
-
-def run_weight_grad(dz, hidden):
+    )(w_blk, z, hidden, lse, targets)
+
+
+def weight_grad_kernel(
+    rows, done, vocab, dz_ref, h_ref, part_ref, dht_ref, loss_in, dw_hbm, dh_hbm, loss_out, buf, dh, osem, csem, hsem
+):
+    i = pl.program_id(0)
+    steps = pl.num_programs(0)
+    slot = lax.rem(i, 2)
+    final = vocab - (done + steps - 1) * rows
+
+    def out_copy(k, size):
+        return pltpu.make_async_copy(
+            buf.at[lax.rem(k, 2), pl.ds(0, size)], dw_hbm.at[pl.ds((done + k) * rows, size)], osem.at[lax.rem(k, 2)]
+        )
+
+    dh_copy = pltpu.make_async_copy(dh, dh_hbm, hsem)
+    part_copy = pltpu.make_async_copy(part_ref, dw_hbm.at[pl.ds(i * rows, rows)], csem)
+
+    @pl.when(i < done)
+    def _():
+        part_copy.start()
+
+    @pl.when(i == 0)
+    def _():
+        loss_out[0] = loss_in[0]
+        dh[...] = dht_ref[...].T
+        dh_copy.start()
+
+    @pl.when(i >= 2)
+    def _():
+        out_copy(i - 2, rows).wait()
+
+    buf[slot] = jnp.dot(dz_ref[...], h_ref[...], preferred_element_type=jnp.float32)
+
+    @pl.when(i < done)
+    def _():
+        part_copy.wait()
+
+    @pl.when(i < steps - 1)
+    def _():
+        out_copy(i, rows).start()
+
+    @pl.when(i == steps - 1)
+    def _():
+        out_copy(i, final).start()
+        out_copy(i - 1, rows).wait()
+        out_copy(i, final).wait()
+        dh_copy.wait()
+
+
+def run_weight_grad(rows, done, dz, hidden, part, dht, loss):
     vocab, tok = dz.shape
-    d = hidden.shape[1]
-    rows = min(ROWS, vocab)
+    d, t = dht.shape
+    steps = pl.cdiv(vocab, rows) - done
+    assert done <= steps and steps >= 2
+    any_spec = pl.BlockSpec(memory_space=pl.ANY)
+    smem_spec = pl.BlockSpec(memory_space=pltpu.SMEM)
     return pl.pallas_call(
-        weight_grad_kernel,
-        grid=(pl.cdiv(vocab, rows),),
+        functools.partial(weight_grad_kernel, rows, done, vocab),
+        grid=(steps,),
         in_specs=[
-            pl.BlockSpec((rows, tok), lambda i: (i, 0)),
+            pl.BlockSpec((rows, tok), lambda i: (done + i, 0)),
             pl.BlockSpec((tok, d), lambda i: (0, 0), pipeline_mode=pl.Buffered(1)),
-        ],
-        out_specs=pl.BlockSpec((rows, d), lambda i: (i, 0)),
-        out_shape=jax.ShapeDtypeStruct((vocab, d), jnp.float32),
+            pl.BlockSpec((rows, d), lambda i: (jnp.minimum(i, done - 1), 0)),
+            pl.BlockSpec((d, t), lambda i: (0, 0), pipeline_mode=pl.Buffered(1)),
+            smem_spec,
+        ],
+        out_specs=[any_spec, any_spec, smem_spec],
+        out_shape=[
+            jax.ShapeDtypeStruct((vocab, d), jnp.float32),
+            jax.ShapeDtypeStruct((t, d), jnp.float32),
+            jax.ShapeDtypeStruct((1,), jnp.float32),
+        ],
+        scratch_shapes=[
+            pltpu.VMEM((2, rows, d), jnp.float32),
+            pltpu.VMEM((t, d), jnp.float32),
+            pltpu.SemaphoreType.DMA((2,)),
+            pltpu.SemaphoreType.DMA,
+            pltpu.SemaphoreType.DMA,
+        ],
         compiler_params=pltpu.CompilerParams(dimension_semantics=("arbitrary",), vmem_limit_bytes=VMEM_LIMIT),
         name="weight_grad",
-    )(dz, hidden)
-
-
-def solution(mesh, tile=TILE):
+    )(dz, hidden, part, dht, loss)
+
+
+def solution(mesh, tile=TILE, rows_w=ROWS):
     n = mesh.shape[AXIS]
 
     def local_step(hidden, targets, w_blk):
         tgt = targets.reshape(n, 1, hidden.shape[0] // n)
         z, lse, loss = run_stats(n, tile, hidden, tgt, w_blk, 0)
-        dht, dz = run_hidden_grad(n, tile, w_blk, z, lse, tgt, 1)
-        return loss[0, :1], dht.T, run_weight_grad(dz, hidden)
+        done = pl.cdiv(w_blk.shape[0], rows_w) // 2
+        dht, dz, part = run_hidden_grad(n, tile, rows_w, done, w_blk, z, hidden, lse, tgt, 1)
+        dw, dh, loss = run_weight_grad(rows_w, done, dz, hidden, part, dht, loss)
+        return loss, dh, dw
 
     return jax.shard_map(
         local_step,

time: 195 us -> 199 us (1.021)
  the two profiles are of different devices: /device:TPU:81 before, /device:TPU:120 now
where the time goes in v3:
time: 199 us
  Pallas kernels  198 us (99%)
    pallas_call x1, Pallas kernels, run_hidden_grad(): pl.pallas_call(functools.partial(hidden_grad_kernel, n, tile, rows_w, blo...  107 us
    pallas_call x1, Pallas kernels, run_stats(): pl.pallas_call(functools.partial(stats_kernel, n, tile), grid=(n,), in_sp...  61.8 us
    pallas_call x1, Pallas kernels, run_weight_grad(): pl.pallas_call(functools.partial(weight_grad_kernel, rows, done, vocab),...  29.7 us

profile of v3, /device:TPU:120, one launch (start us, length us, event | category | flops | bytes accessed | tf_op | source)
XLA Modules:
  0.0 198.9 jit_solution(4798016273724309257)
XLA Ops:
  0.6 61.8 %stats.1 = (f32[8,6288,512]{2,1,0:T(8,128)}, f32[8,1,512]{2,1,0:T(1,128)}, f32[1]{0:T(128)}) custom-call(bf16[4096,768]{1,0:T(8,128)(2,1)} %h_ref.3, bf16[6288,768]{1,0:T(8,128)(2,1)} %w_hbm.3, s32[8,1,512]{2,1,0:T(1,128)} %bitcast.1), custom_call_target="tpu_custom_call" | custom-call | tf_op jit(solution)/shard_map/stats/pallas_call | solution.py:132
  62.5 106.6 %hidden_grad.1 = (f32[768,512]{1,0:T(8,128)}, bf16[6288,4096]{1,0:T(8,128)(2,1)}, f32[3168,768]{1,0:T(8,128)}) custom-call(bf16[6288,768]{1,0:T(8,128)(2,1)} %w_hbm.3, f32[8,6288,512]{2,1,0:T(8,128)} %get-tuple-element.12.z_hbm, bf16[4096,768]{1,0:T(8,128)(2,1)} %h_ref.3, f32[8,1,512]{2,1,0:T(1,128)} %get-tuple-element.13.lse_ref, s32[8,1,512]{2,1,0:T(1,128)} %bitcast.2), custom_call_target="tpu_custom_call" | custom-call | tf_op jit(solution)/shard_map/hidden_grad/pallas_call | solution.py:377
  169.1 29.7 %weight_grad.1 = (f32[6288,768]{1,0:T(8,128)}, f32[512,768]{1,0:T(8,128)}, f32[1]{0:T(128)}) custom-call(bf16[6288,4096]{1,0:T(8,128)(2,1)} %get-tuple-element.14.dz_ref, bf16[4096,768]{1,0:T(8,128)(2,1)} %h_ref.3, f32[3168,768]{1,0:T(8,128)} %get-tuple-element.15.part_ref, f32[768,512]{1,0:T(8,128)} %get-tuple-element.16.dht_ref, f32[1]{0:T(128)} %get-tuple-element.17.loss_in), custom_call_target="tpu_custom_call" | custom-call | tf_op jit(solution)/shard_map/weight_grad/pallas_call | solution.py:469

commit v4 on v3

--- a/solution.py
+++ b/solution.py
@@ -93,9 +93,6 @@
     @pl.when(c == n - 1)
     def _():
         send(c)
-        pltpu.make_async_copy(zbuf.at[1 - p], z_hbm.at[c - 1], zsem.at[1 - p]).wait()
-        pltpu.make_async_copy(zbuf.at[p], z_hbm.at[c], zsem.at[p]).wait()
-        pltpu.make_async_copy(recv, recv, send_sem).wait()
         pltpu.make_async_copy(recv, recv, recv_sem).wait()
         total = jnp.float32(0.0)
         for k in range(n):
@@ -112,6 +109,9 @@
             lse_ref[k] = lse
             total = total + jnp.sum(lse - target)
         loss_ref[0] = total * (1.0 / (n * t))
+        pltpu.make_async_copy(recv, recv, send_sem).wait()
+        pltpu.make_async_copy(zbuf.at[1 - p], z_hbm.at[c - 1], zsem.at[1 - p]).wait()
+        pltpu.make_async_copy(zbuf.at[p], z_hbm.at[c], zsem.at[p]).wait()
 
 
 def stat_sum(n, me, own, parts):
@@ -186,7 +186,7 @@
 
     def chunk_of(s):
         q, mine = lax.div(s, 2), lax.rem(s, 2)
-        e = sgn * (2 * mine - 1)
+        e = sgn * (1 - 2 * mine)
         off = jnp.where(q == 0, 2, jnp.where(q == 1, e, jnp.where(q == 2, -e, 0)))
         owner_core = core * mine + (1 - core) * (1 - mine)
         return 2 * lax.rem(x + off + nx, nx) + owner_core
@@ -213,7 +213,7 @@
 
     def ring_copy(q, peer):
         return pltpu.make_async_remote_copy(
-            src_ref=hacc.at[1 + lax.rem(q, 2)], dst_ref=from_ring.at[q], send_sem=r_send.at[q], recv_sem=r_recv.at[q],
+            src_ref=hacc.at[1 + q], dst_ref=from_ring.at[q], send_sem=r_send.at[q], recv_sem=r_recv.at[q],
             device_id={AXIS: peer}, device_id_type=MESH,
         )
 
@@ -244,18 +244,14 @@
     def stage(s, carry):
         chunk, following = chunk_of(s), chunk_of(jnp.minimum(s + 1, n - 1))
         q, mine = lax.div(s, 2), lax.rem(s, 2)
-        acc = mine * (1 + lax.rem(q, 2))
+        acc = mine * (1 + q)
         pq, pmine = lax.div(s - 1, 2), lax.rem(s + 1, 2)
-        pacc = 1 + lax.rem(pq, 2)
+        pacc = 1 + pq
         lse, tgt = lse_ref[chunk], tgt_ref[chunk] - me * vocab
 
         @pl.when(jnp.logical_and(mine == 0, q >= 1))
         def _():
             partner_copy(q - 1).wait_send()
-
-        @pl.when(jnp.logical_and(mine == 1, q >= 2))
-        def _():
-            ring_copy(q - 2, ahead).wait_send()
 
         for j, (r0, rows) in enumerate(tiles):
             z_copy(chunk, j).wait()
@@ -308,10 +304,10 @@
                     partner_copy(pq).wait_recv()
                     hacc[pacc] = hacc[pacc] + from_partner[pq]
 
-                @pl.when(s == 5)
+                @pl.when(s == 7)
                 def _():
                     ring_copy(0, ahead).wait_recv()
-                    hacc[2] = hacc[2] + from_ring[0]
+                    hacc[3] = hacc[3] + from_ring[0]
 
             if j == 1:
 
@@ -323,13 +319,13 @@
                 def _():
                     ring_copy(0, ahead).start()
 
-                @pl.when(s == 5)
-                def _():
-                    ring_copy(1, ahead).start()
-
-                @pl.when(s == 6)
-                def _():
-                    ring_copy(2, behind).start()
+                @pl.when(s == 4)
+                def _():
+                    ring_copy(1, behind).start()
+
+                @pl.when(s == 7)
+                def _():
+                    ring_copy(2, ahead).start()
 
         return carry
 
@@ -357,13 +353,14 @@
 
     lax.fori_loop(0, blocks_w, block, 0)
     partner_copy(3).wait_recv()
-    total = hacc[2] + from_partner[3]
-    ring_copy(1, ahead).wait_recv()
-    total = total + from_ring[1]
-    ring_copy(2, behind).wait_recv()
+    ring_copy(1, behind).wait_recv()
+    total = hacc[4] + from_partner[3] + from_ring[1]
+    ring_copy(2, ahead).wait_recv()
     dht_ref[...] = total + from_ring[2]
     partner_copy(3).wait_send()
-    ring_copy(2, behind).wait_send()
+    ring_copy(0, ahead).wait_send()
+    ring_copy(1, behind).wait_send()
+    ring_copy(2, ahead).wait_send()
     for i in range(max(blocks_w - 2, 0), blocks_w):
         dw_copy(i).wait()
 
@@ -387,7 +384,7 @@
             pltpu.VMEM((vocab, d), jnp.bfloat16),
             pltpu.VMEM((3, rows, t), jnp.float32),
             pltpu.VMEM((3, rows, t), jnp.bfloat16),
-            pltpu.VMEM((3, d, t), jnp.float32),
+            pltpu.VMEM((5, d, t), jnp.float32),
             pltpu.VMEM((4, d, t), jnp.float32),
             pltpu.VMEM((3, d, t), jnp.float32),
             pltpu.VMEM((n * t, d), jnp.bfloat16),
@@ -412,7 +409,8 @@
 
 
 def weight_grad_kernel(
-    rows, done, vocab, dz_ref, h_ref, part_ref, dht_ref, loss_in, dw_hbm, dh_hbm, loss_out, buf, dh, osem, csem, hsem
+    rows, done, vocab, dz_ref, h_ref, part_ref, dht_hbm, loss_in, dw_hbm, dh_hbm, loss_out,
+    buf, dht, dh, osem, csem, hsem,
 ):
     i = pl.program_id(0)
     steps = pl.num_programs(0)
@@ -424,6 +422,7 @@
             buf.at[lax.rem(k, 2), pl.ds(0, size)], dw_hbm.at[pl.ds((done + k) * rows, size)], osem.at[lax.rem(k, 2)]
         )
 
+    dht_copy = pltpu.make_async_copy(dht_hbm, dht, hsem)
     dh_copy = pltpu.make_async_copy(dh, dh_hbm, hsem)
     part_copy = pltpu.make_async_copy(part_ref, dw_hbm.at[pl.ds(i * rows, rows)], csem)
 
@@ -434,7 +433,12 @@
     @pl.when(i == 0)
     def _():
         loss_out[0] = loss_in[0]
-        dh[...] = dht_ref[...].T
+        dht_copy.start()
+
+    @pl.when(i == 1)
+    def _():
+        dht_copy.wait()
+        dh[...] = dht[...].T
         dh_copy.start()
 
     @pl.when(i >= 2)
@@ -473,7 +477,7 @@
             pl.BlockSpec((rows, tok), lambda i: (done + i, 0)),
             pl.BlockSpec((tok, d), lambda i: (0, 0), pipeline_mode=pl.Buffered(1)),
             pl.BlockSpec((rows, d), lambda i: (jnp.minimum(i, done - 1), 0)),
-            pl.BlockSpec((d, t), lambda i: (0, 0), pipeline_mode=pl.Buffered(1)),
+            any_spec,
             smem_spec,
         ],
         out_specs=[any_spec, any_spec, smem_spec],
@@ -484,6 +488,7 @@
         ],
         scratch_shapes=[
             pltpu.VMEM((2, rows, d), jnp.float32),
+            pltpu.VMEM((d, t), jnp.float32),
             pltpu.VMEM((t, d), jnp.float32),
             pltpu.SemaphoreType.DMA((2,)),
             pltpu.SemaphoreType.DMA,

time: 199 us -> 180 us (0.905)
  the two profiles are of different devices: /device:TPU:120 before, /device:TPU:81 now
where the time goes in v4:
time: 180 us; the launch traced here: 179 us
  Pallas kernels  179 us (99%)
    pallas_call x1, Pallas kernels, run_hidden_grad(): pl.pallas_call(functools.partial(hidden_grad_kernel, n, tile, rows_w, blo...  86.2 us
    pallas_call x1, Pallas kernels, run_stats(): pl.pallas_call(functools.partial(stats_kernel, n, tile), grid=(n,), in_sp...  63 us
    pallas_call x1, Pallas kernels, run_weight_grad(): pl.pallas_call(functools.partial(weight_grad_kernel, rows, done, vocab),...  29.4 us

profile of v4, /device:TPU:81, one launch (start us, length us, event | category | flops | bytes accessed | tf_op | source)
XLA Modules:
  0.0 179.3 jit_solution(17338202561702987849)
XLA Ops:
  0.6 63.0 %stats.1 = (f32[8,6288,512]{2,1,0:T(8,128)}, f32[8,1,512]{2,1,0:T(1,128)}, f32[1]{0:T(128)}) custom-call(bf16[4096,768]{1,0:T(8,128)(2,1)} %h_ref.3, bf16[6288,768]{1,0:T(8,128)(2,1)} %w_hbm.3, s32[8,1,512]{2,1,0:T(1,128)} %bitcast.1), custom_call_target="tpu_custom_call" | custom-call | tf_op jit(solution)/shard_map/stats/pallas_call | solution.py:132
  63.6 86.2 %hidden_grad.1 = (f32[768,512]{1,0:T(8,128)}, bf16[6288,4096]{1,0:T(8,128)(2,1)}, f32[3168,768]{1,0:T(8,128)}) custom-call(bf16[6288,768]{1,0:T(8,128)(2,1)} %w_hbm.3, f32[8,6288,512]{2,1,0:T(8,128)} %get-tuple-element.12.z_hbm, bf16[4096,768]{1,0:T(8,128)(2,1)} %h_ref.3, f32[8,1,512]{2,1,0:T(1,128)} %get-tuple-element.13.lse_ref, s32[8,1,512]{2,1,0:T(1,128)} %bitcast.2), custom_call_target="tpu_custom_call" | custom-call | tf_op jit(solution)/shard_map/hidden_grad/pallas_call | solution.py:374
  149.7 29.4 %weight_grad.1 = (f32[6288,768]{1,0:T(8,128)}, f32[512,768]{1,0:T(8,128)}, f32[1]{0:T(128)}) custom-call(bf16[6288,4096]{1,0:T(8,128)(2,1)} %get-tuple-element.14.dz_ref, bf16[4096,768]{1,0:T(8,128)(2,1)} %h_ref.3, f32[3168,768]{1,0:T(8,128)} %get-tuple-element.15.part_ref, f32[768,512]{1,0:T(8,128)} %get-tuple-element.16.dht_hbm, f32[1]{0:T(128)} %get-tuple-element.17.loss_in), custom_call_target="tpu_custom_call" | custom-call | tf_op jit(solution)/shard_map/weight_grad/pallas_call | solution.py:473
